TPU v7x, 32 devices: a whole 2x2x4 slice. The times are simulated.
32 devices in a mesh: dp: 8 (over z, x), owner: 4 (over y, core).
Axes of the slice: x: 2, y: 2, z: 4, core: 2. Of those that a mesh axis runs over, the one named last changes fastest.
Arguments:
- gradients: float32 [8, 1024, 7168], P(None, 'dp', 'owner'), may hold values from -6 to 6
- rows_live: int32 [8], replicated, may hold values from 256 to 1024
Outputs:
- updates: bfloat16 [8, 1024, 7168], P(None, 'dp', 'owner')
All inputs are finite; a program needn't handle non-finite values.
Results may differ from a plain program's by a relative error of at most 0.015.
Values may be sent and summed in bfloat16 or wider, within the bound.
A program may use at most 64 MiB of HBM per device.

v0:
```python
import math
import jax
import jax.numpy as jnp
from jax import lax
from jax.sharding import PartitionSpec as P

D = 7168


def body(gradients, rows_live):
    narrowed = gradients.astype(jnp.bfloat16)
    regrouped = lax.all_to_all(narrowed, "dp", split_axis=0, concat_axis=1, tiled=True)
    owned_count = regrouped.shape[0]
    hidden_rows = regrouped.shape[1]
    first_owned = lax.axis_index("dp") * owned_count
    live_counts = lax.dynamic_slice_in_dim(rows_live, first_owned, owned_count)
    live_mask = jnp.arange(hidden_rows, dtype=jnp.int32)[None, :, None] < live_counts[:, None, None]
    regrouped = jnp.where(live_mask, regrouped, jnp.zeros_like(regrouped))
    partial_gram = jnp.einsum(
        "mcr,mdr->mcd", regrouped, regrouped, preferred_element_type=jnp.float32
    )
    live_float = live_counts.astype(jnp.float32)
    whole_gram = lax.psum(partial_gram.astype(jnp.bfloat16), "owner").astype(jnp.float32)
    trace_total = jnp.trace(whole_gram, axis1=1, axis2=2)
    scale_sq = 2.0 * trace_total / live_float
    normed_gram = (whole_gram / scale_sq[:, None, None]).astype(jnp.bfloat16)
    inverse = (1.0 / jnp.sqrt(scale_sq))[:, None, None]
    once = (
        jnp.einsum("mcd,mdr->mcr", normed_gram, regrouped, preferred_element_type=jnp.float32)
        * inverse
    )
    twice = jnp.einsum(
        "mcd,mdr->mcr", normed_gram, once.astype(jnp.bfloat16), preferred_element_type=jnp.float32
    )
    combined = 3.4445 * regrouped.astype(jnp.float32) * inverse - 4.775 * once + 2.0315 * twice
    update_rows = (combined * (0.2 * math.sqrt(D))).astype(jnp.bfloat16)
    return lax.all_to_all(update_rows, "dp", split_axis=1, concat_axis=0, tiled=True)


def solution(mesh):
    return jax.shard_map(
        body,
        mesh=mesh,
        in_specs=(P(None, "dp", "owner"), P()),
        out_specs=P(None, "dp", "owner"),
        check_vma=False,
    )
```

profile of v0, /device:TPU:0, one launch (start us, length us, event | category | flops | bytes accessed | tf_op | source)
XLA Modules:
  0.0 389.9 jit_solution(16820926485267107496)
XLA Ops:
  6.5 5.3 %convert_element_type.32 = bf16[8,128,1792]{2,1,0:T(8,128)(2,1)} convert(f32[8,128,1792]{2,1,0:T(8,128)} %param.2) | non-fusion elementwise | flops 1835008 | bytes 11010048 | tf_op jit(solution)/shard_map/convert_element_type | solution.py:11
  11.9 0.0 copy-start.2
  11.9 7.4 %all-to-all-start = ((bf16[8,128,1792]{2,1,0:T(8,128)(2,1)}), bf16[8,128,1792]{2,1,0:T(8,128)(2,1)}, u32[]{:S(2)}, u32[]{:S(2)}) async-start(bf16[8,128,1792]{2,1,0:T(8,128)(2,1)} %convert_element_type.32), calls=%async_computation | async-start | bytes 7340032 | tf_op jit(solution)/shard_map/all_to_all | solution.py:12
  19.3 0.0 all-reduce.2.cloned.1.call-start
  19.3 0.0 copy-done.2
  19.3 0.6 dynamic_slice.3
  19.9 0.6 iota_compare_fusion.1
  20.6 80.8 %all-to-all-done = bf16[8,128,1792]{2,1,0:T(8,128)(2,1)} async-done(((bf16[8,128,1792]{2,1,0:T(8,128)(2,1)}), bf16[8,128,1792]{2,1,0:T(8,128)(2,1)}, u32[]{:S(2)}, u32[]{:S(2)}) %all-to-all-start) | async-done | bytes 3670048 | tf_op jit(solution)/shard_map/all_to_all | solution.py:12
  101.3 8.6 %convert_bitcast_fusion = bf16[1,1024,1024]{2,1,0:T(8,128)(2,1)} fusion(bf16[1,1024,1,1,1,1,1792]{6,1,5,4,3,2,0:T(8,128)(2,1)} %bitcast.2, pred[1024]{0:T(1024)(128)(4,1)S(1)} %iota_compare_fusion.1), kind=kOutput, calls=%fused_computation.16 | convolution fusion | flops 3760979968 | bytes 5768192 | tf_op jit(solution)/shard_map/mcr,mdr->mcd/dot_general | solution.py:19
  109.9 0.0 all-reduce.2.cloned.1.call-update
  110.5 4.2 %bitcast_select_fusion = bf16[1024,1792]{1,0:T(8,128)(2,1)} fusion(bf16[8,128,1792]{2,1,0:T(8,128)(2,1)} %all-to-all-done, pred[1024]{0:T(1024)(128)(4,1)S(1)} %iota_compare_fusion.1), kind=kLoop, calls=%fused_computation.11 | loop fusion | flops 1835008 | bytes 7341056 | tf_op jit(solution)/shard_map/jit(_where)/select_n | solution.py:18
  114.7 45.8 %all-reduce.2.cloned.1.call-done = bf16[1,1024,1024]{2,1,0:T(8,128)(2,1)} async-done(((bf16[1,1024,1024]{2,1,0:T(8,128)(2,1)}), bf16[1,1024,1024]{2,1,0:T(8,128)(2,1)}) %all-reduce.2.cloned.1.call-update) | async-done | bytes 2097168 | tf_op jit(solution)/shard_map/psum | solution.py:23
  160.6 2.4 fusion
  163.7 0.0 copy-start
  163.8 0.0 copy-start.1
  163.8 9.9 %fusion.2 = f32[1024,1792]{1,0:T(8,128)} fusion(bf16[1,1024,1,1,1,1,1792]{6,1,5,4,3,2,0:T(8,128)(2,1)} %bitcast.2, pred[1024]{0:T(1024)(128)(4,1)S(1)} %iota_compare_fusion.1, bf16[1,1024,1024]{2,1,0:T(8,128)(2,1)} %all-reduce.2.cloned.1.call-done, f32[]{:T(128)} %bitcast.7), kind=kOutput, calls=%fused_computation.7 | convolution fusion | flops 3763077120 | bytes 13108228 | tf_op jit(solution)/shard_map/mcd,mdr->mcr/dot_general | solution.py:29
  173.6 0.0 copy-done
  173.6 0.0 copy-done.1
  173.6 10.1 %fusion.7 = bf16[1,1024,1792]{2,1,0:T(8,128)(2,1)S(1)} fusion(f32[1024,1792]{1,0:T(8,128)} %fusion.2, f32[]{:T(128)} %bitcast.6, f32[]{:T(128)S(6)} %mul.54, bf16[1024,1792]{1,0:T(8,128)(2,1)S(1)} %copy-done, bf16[1,1024,1024]{2,1,0:T(8,128)(2,1)S(1)} %copy-done.1, f32[]{:T(128)} %bitcast.7), kind=kOutput, calls=%fused_computation.14 | convolution fusion | flops 3781427200 | bytes 16777228 | tf_op jit(solution)/shard_map/mcd,mdr->mcr/dot_general | solution.py:32
  183.8 52.2 %copy.7 = bf16[1,1024,1792]{2,0,1:T(2,128)(2,1)} copy(bf16[1,1024,1792]{2,1,0:T(8,128)(2,1)S(1)} %fusion.7) | data formatting | bytes 7340032 | tf_op jit(solution)/shard_map/convert_element_type | solution.py:36
  236.0 0.6 broadcast.60
  236.6 38.7 %reduce.1 = bf16[1024,1792]{1,0:T(8,128)(2,1)} reduce(bf16[1024,1,1792]{2,1,0:T(2,128)(2,1)} %bitcast.27, bf16[]{:T(256)} %broadcast.60), dimensions={1}, to_apply=%bitcast.26.reduce_sub_computation | reduce | bytes 7340034
  275.2 6.6 %reshape.127 = bf16[8,2,114688]{2,1,0:T(2,128)(2,1)} reshape(bf16[1024,1792]{1,0:T(8,128)(2,1)} %reduce.1) | data formatting | bytes 7340032
  281.8 87.5 %all_to_all.27 = bf16[8,2,114688]{2,1,0:T(2,128)(2,1)} all-to-all(bf16[8,2,114688]{2,1,0:T(2,128)(2,1)} %reshape.127), channel_id=1, replica_groups=mesh['dp'=8,'owner'=4] {'dp'}, dimensions={0} | all-to-all | bytes 7340032 | tf_op jit(solution)/shard_map/all_to_all | solution.py:37
  369.3 8.3 %reshape.128 = bf16[1024,1,1792]{2,1,0:T(2,128)(2,1)} reshape(bf16[8,2,114688]{2,1,0:T(2,128)(2,1)} %all_to_all.27) | data formatting | bytes 7340032
  377.6 5.5 %copy.5 = bf16[1,1024,1792]{2,1,0:T(8,128)(2,1)} copy(bf16[1,1024,1792]{2,0,1:T(2,128)(2,1)} %bitcast.28) | data formatting | bytes 7340032
Async XLA Ops:
  11.9 7.5 %copy-start.2 = (s32[8]{0:T(128)S(1)}, s32[8]{0:T(128)}, u32[]{:S(2)}) copy-start(s32[8]{0:T(128)} %param.3) | copy-start | bytes 100
  11.9 89.5 %all-to-all-start = ((bf16[8,128,1792]{2,1,0:T(8,128)(2,1)}), bf16[8,128,1792]{2,1,0:T(8,128)(2,1)}, u32[]{:S(2)}, u32[]{:S(2)}) async-start(bf16[8,128,1792]{2,1,0:T(8,128)(2,1)} %convert_element_type.32), calls=%async_computation | async-start | bytes 7340032 | tf_op jit(solution)/shard_map/all_to_all | solution.py:12
  19.3 141.3 %all-reduce.2.cloned.1.call-start = ((), (), s32[]{:S(2)}) async-start(), calls=%async_computation.2 | async-start | bytes 4194304 | tf_op jit(solution)/shard_map/psum | solution.py:23
  163.7 9.9 %copy-start = (bf16[1024,1792]{1,0:T(8,128)(2,1)S(1)}, bf16[1024,1792]{1,0:T(8,128)(2,1)}, u32[]{:S(2)}) copy-start(bf16[1024,1792]{1,0:T(8,128)(2,1)} %bitcast_select_fusion) | copy-start | bytes 11010052
  163.8 9.9 %copy-start.1 = (bf16[1,1024,1024]{2,1,0:T(8,128)(2,1)S(1)}, bf16[1,1024,1024]{2,1,0:T(8,128)(2,1)}, u32[]{:S(2)}) copy-start(bf16[1,1024,1024]{2,1,0:T(8,128)(2,1)} %all-reduce.2.cloned.1.call-done) | copy-start | bytes 6291460
Sparse Core Ops, SparseCore 0:
  110.0 50.4 all-reduce.1
where the time goes:
time: 391 us; the launch traced here: 390 us
  waiting for transfers between devices  127 us (32%)
  blocking collectives  87.5 us (22%)
  local copies, waits for them, and re-layouts  73.8 us (19%)
  other arithmetic  51.2 us (13%)
  matrix products  28.5 us (7%)
  between operations  14.8 us (4%)
  starting transfers between devices  7.45 us (2%)
    all_to_all x1, blocking collectives, body(): lax.all_to_all(update_rows, 'dp', split_axis=1, concat_axis=0, tiled=True)  87.5 us
    all_to_all x1, waiting for transfers between devices, body(): lax.all_to_all(narrowed, 'dp', split_axis=0, concat_axis=1, tiled=True)  80.8 us
    convert_element_type x1, local copies, waits for them, and re-layouts, body(): update_rows = (combined * (0.2 * math.sqrt(D))).astype(jnp.bfloat16)  52.2 us
    psum x1, waiting for transfers between devices, body(): lax.psum(partial_gram.astype(jnp.bfloat16), 'owner').astype(jnp.float32)  45.8 us
    unnamed x1, other arithmetic  38.7 us
    unnamed x10, local copies, waits for them, and re-layouts  21 us
    dot_general x1, matrix products, body(): jnp.einsum('mcd,mdr->mcr', normed_gram, once.astype(jnp.bfloat16), prefer...  10.1 us
    dot_general x1, matrix products, body(): jnp.einsum('mcd,mdr->mcr', normed_gram, regrouped, preferred_element_type...  9.87 us
  transfers between devices with their start and end apart: 2, of which 2 were waited for; matrix products, arithmetic and copies ran while one was open for 1% of the time, Pallas kernels for 0%

commit v1 on v0

--- a/solution.py
+++ b/solution.py
@@ -20,7 +20,9 @@
         "mcr,mdr->mcd", regrouped, regrouped, preferred_element_type=jnp.float32
     )
     live_float = live_counts.astype(jnp.float32)
-    whole_gram = lax.psum(partial_gram.astype(jnp.bfloat16), "owner").astype(jnp.float32)
+    whole_gram = jnp.sum(lax.all_gather(partial_gram.astype(jnp.bfloat16), "owner"), axis=0).astype(
+        jnp.float32
+    )
     trace_total = jnp.trace(whole_gram, axis1=1, axis2=2)
     scale_sq = 2.0 * trace_total / live_float
     normed_gram = (whole_gram / scale_sq[:, None, None]).astype(jnp.bfloat16)

time: 391 us -> 402 us (1.028)
  waiting for transfers between devices: 127 us -> 133 us
  other arithmetic: 51.2 us -> 56.1 us
    all_gather x0 -> x1, waiting for transfers between devices: none -> 52.7 us  [body(): lax.all_gather(partial_gram.astype(jnp.bfloat16), 'owner')]
    psum x1 -> x0, waiting for transfers between devices: 45.8 us -> none  [body(): lax.psum(partial_gram.astype(jnp.bfloat16), 'owner').astype(jnp.float32)]
    reduce_sum x0 -> x1, other arithmetic: none -> 6.5 us  [body(): jnp.sum(lax.all_gather(partial_gram.astype(jnp.bfloat16), 'owner'), axis=0)]
    unnamed x10 -> x6, local copies, waits for them, and re-layouts: 21 us -> 21 us
where the time goes in v1:
time: 402 us; the launch traced here: 401 us
  waiting for transfers between devices  133 us (33%)
  blocking collectives  87.9 us (22%)
  local copies, waits for them, and re-layouts  73.8 us (18%)
  other arithmetic  56.1 us (14%)
  matrix products  27.8 us (7%)
  between operations  14.8 us (4%)
  starting transfers between devices  7.45 us (2%)
    all_to_all x1, blocking collectives, body(): lax.all_to_all(update_rows, 'dp', split_axis=1, concat_axis=0, tiled=True)  87.9 us
    all_to_all x1, waiting for transfers between devices, body(): lax.all_to_all(narrowed, 'dp', split_axis=0, concat_axis=1, tiled=True)  80.7 us
    all_gather x1, waiting for transfers between devices, body(): lax.all_gather(partial_gram.astype(jnp.bfloat16), 'owner')  52.7 us
    convert_element_type x1, local copies, waits for them, and re-layouts, body(): update_rows = (combined * (0.2 * math.sqrt(D))).astype(jnp.bfloat16)  52.2 us
    unnamed x1, other arithmetic  38.7 us
    unnamed x6, local copies, waits for them, and re-layouts  21 us
    dot_general x1, matrix products, body(): jnp.einsum('mcd,mdr->mcr', normed_gram, once.astype(jnp.bfloat16), prefer...  10.9 us
    dot_general x1, matrix products, body(): jnp.einsum('mcr,mdr->mcd', regrouped, regrouped, preferred_element_type=j...  8.67 us
  transfers between devices with their start and end apart: 2, of which 2 were waited for; matrix products, arithmetic and copies ran while one was open for 1% of the time, Pallas kernels for 0%

profile of v1, /device:TPU:0, one launch (start us, length us, event | category | flops | bytes accessed | tf_op | source)
XLA Modules:
  0.0 401.4 jit_solution(11375566652631260556)
XLA Ops:
  6.5 5.3 %convert_element_type.52 = bf16[8,128,1792]{2,1,0:T(8,128)(2,1)} convert(f32[8,128,1792]{2,1,0:T(8,128)} %param.2) | non-fusion elementwise | flops 1835008 | bytes 11010048 | tf_op jit(solution)/shard_map/convert_element_type | solution.py:11
  11.9 0.0 copy-start
  11.9 7.4 %all-to-all-start = ((bf16[8,128,1792]{2,1,0:T(8,128)(2,1)}), bf16[8,128,1792]{2,1,0:T(8,128)(2,1)}, u32[]{:S(2)}, u32[]{:S(2)}) async-start(bf16[8,128,1792]{2,1,0:T(8,128)(2,1)} %convert_element_type.52), calls=%async_computation | async-start | bytes 7340032 | tf_op jit(solution)/shard_map/all_to_all | solution.py:12
  19.3 0.0 all-gather.3.cloned.1.call-start
  19.3 0.0 copy-done
  19.3 0.6 dynamic_slice.3
  20.0 0.6 iota_compare_fusion.1
  20.6 80.7 %all-to-all-done = bf16[8,128,1792]{2,1,0:T(8,128)(2,1)} async-done(((bf16[8,128,1792]{2,1,0:T(8,128)(2,1)}), bf16[8,128,1792]{2,1,0:T(8,128)(2,1)}, u32[]{:S(2)}, u32[]{:S(2)}) %all-to-all-start) | async-done | bytes 3670048 | tf_op jit(solution)/shard_map/all_to_all | solution.py:12
  101.3 8.7 %fusion.8 = bf16[1024,1024]{1,0:T(8,128)(2,1)} fusion(bf16[1,1024,1,1,1,1,1792]{6,1,5,4,3,2,0:T(8,128)(2,1)} %bitcast.2, pred[1024]{0:T(1024)(128)(4,1)S(1)} %iota_compare_fusion.1), kind=kOutput, calls=%fused_computation.14 | convolution fusion | flops 3760979968 | bytes 5768192 | tf_op jit(solution)/shard_map/mcr,mdr->mcd/dot_general | solution.py:19
  110.0 0.0 all-gather.3.cloned.1.call-update
  110.7 4.2 %bitcast_select_fusion = bf16[1024,1792]{1,0:T(8,128)(2,1)} fusion(bf16[8,128,1792]{2,1,0:T(8,128)(2,1)} %all-to-all-done, pred[1024]{0:T(1024)(128)(4,1)S(1)} %iota_compare_fusion.1), kind=kLoop, calls=%fused_computation.9 | loop fusion | flops 1835008 | bytes 7341056 | tf_op jit(solution)/shard_map/jit(_where)/select_n | solution.py:18
  114.9 52.7 %all-gather.3.cloned.1.call-done = bf16[4096,1024]{1,0:T(8,128)(2,1)} async-done(((bf16[1024,1024]{1,0:T(8,128)(2,1)}), bf16[4096,1024]{1,0:T(8,128)(2,1)}) %all-gather.3.cloned.1.call-update) | async-done | bytes 8388624 | tf_op jit(solution)/shard_map/all_gather | solution.py:23
  167.5 6.5 %reduce.3 = bf16[1024,1024]{1,0:T(8,128)(2,1)S(1)} reduce(bf16[4,1024,1024]{2,1,0:T(8,128)(2,1)} %bitcast.23, bf16[]{:T(256)} %constant.7.clone.1), dimensions={0}, to_apply=%region_0.1 | reduce | flops 3145728 | bytes 10485762 | tf_op jit(solution)/shard_map/reduce_sum | solution.py:23
  174.0 0.8 fusion
  175.6 8.2 %fusion.14 = f32[1024,1792]{1,0:T(8,128)} fusion(bf16[1024,1792]{1,0:T(8,128)(2,1)} %bitcast_select_fusion, bf16[1024,1024]{1,0:T(8,128)(2,1)S(1)} %reduce.3, f32[]{:T(128)} %bitcast.7), kind=kOutput, calls=%fused_computation.18 | convolution fusion | flops 3761242112 | bytes 13107204 | tf_op jit(solution)/shard_map/mcd,mdr->mcr/dot_general | solution.py:31
  183.8 10.9 %fusion.7 = bf16[1,1024,1792]{2,1,0:T(8,128)(2,1)S(1)} fusion(f32[1024,1792]{1,0:T(8,128)} %fusion.14, f32[]{:T(128)} %bitcast.6, f32[]{:T(128)S(6)} %mul.54, bf16[1024,1792]{1,0:T(8,128)(2,1)} %bitcast_select_fusion, bf16[1024,1024]{1,0:T(8,128)(2,1)S(1)} %reduce.3, f32[]{:T(128)} %bitcast.7), kind=kOutput, calls=%fused_computation.13 | convolution fusion | flops 3781427200 | bytes 16777228 | tf_op jit(solution)/shard_map/mcd,mdr->mcr/dot_general | solution.py:34
  194.8 52.2 %copy.8 = bf16[1,1024,1792]{2,0,1:T(2,128)(2,1)} copy(bf16[1,1024,1792]{2,1,0:T(8,128)(2,1)S(1)} %fusion.7) | data formatting | bytes 7340032 | tf_op jit(solution)/shard_map/convert_element_type | solution.py:38
  247.0 0.6 broadcast.70
  247.6 38.7 %reduce.4 = bf16[1024,1792]{1,0:T(8,128)(2,1)} reduce(bf16[1024,1,1792]{2,1,0:T(2,128)(2,1)} %bitcast.21, bf16[]{:T(256)} %broadcast.70), dimensions={1}, to_apply=%bitcast.20.reduce_sub_computation | reduce | bytes 7340034
  286.2 6.6 %reshape.129 = bf16[8,2,114688]{2,1,0:T(2,128)(2,1)} reshape(bf16[1024,1792]{1,0:T(8,128)(2,1)} %reduce.4) | data formatting | bytes 7340032
  292.9 87.9 %all_to_all.27 = bf16[8,2,114688]{2,1,0:T(2,128)(2,1)} all-to-all(bf16[8,2,114688]{2,1,0:T(2,128)(2,1)} %reshape.129), channel_id=1, replica_groups=mesh['dp'=8,'owner'=4] {'dp'}, dimensions={0} | all-to-all | bytes 7340032 | tf_op jit(solution)/shard_map/all_to_all | solution.py:39
  380.8 8.3 %reshape.130 = bf16[1024,1,1792]{2,1,0:T(2,128)(2,1)} reshape(bf16[8,2,114688]{2,1,0:T(2,128)(2,1)} %all_to_all.27) | data formatting | bytes 7340032
  389.1 5.5 %copy.6 = bf16[1,1024,1792]{2,1,0:T(8,128)(2,1)} copy(bf16[1,1024,1792]{2,0,1:T(2,128)(2,1)} %bitcast.22) | data formatting | bytes 7340032
Async XLA Ops:
  11.9 7.5 %copy-start = (s32[8]{0:T(128)S(1)}, s32[8]{0:T(128)}, u32[]{:S(2)}) copy-start(s32[8]{0:T(128)} %param.3) | copy-start | bytes 100
  11.9 89.5 %all-to-all-start = ((bf16[8,128,1792]{2,1,0:T(8,128)(2,1)}), bf16[8,128,1792]{2,1,0:T(8,128)(2,1)}, u32[]{:S(2)}, u32[]{:S(2)}) async-start(bf16[8,128,1792]{2,1,0:T(8,128)(2,1)} %convert_element_type.52), calls=%async_computation | async-start | bytes 7340032 | tf_op jit(solution)/shard_map/all_to_all | solution.py:12
  19.3 148.2 %all-gather.3.cloned.1.call-start = ((), (), s32[]{:S(2)}) async-start(), calls=%async_computation.2 | async-start | bytes 10485760 | tf_op jit(solution)/shard_map/all_gather | solution.py:23
Sparse Core Ops, SparseCore 0:
  110.2 57.3 all-gather.2

commit v2 on v0

--- a/solution.py
+++ b/solution.py
@@ -34,7 +34,10 @@
     )
     combined = 3.4445 * regrouped.astype(jnp.float32) * inverse - 4.775 * once + 2.0315 * twice
     update_rows = (combined * (0.2 * math.sqrt(D))).astype(jnp.bfloat16)
-    return lax.all_to_all(update_rows, "dp", split_axis=1, concat_axis=0, tiled=True)
+    return jnp.concatenate(
+        lax.all_to_all(jnp.stack(jnp.split(update_rows, lax.axis_size("dp"), axis=1)), "dp", 0, 0),
+        axis=0,
+    )
 
 
 def solution(mesh):

time: 391 us -> 280 us (0.72)
  local copies, waits for them, and re-layouts: 73.8 us -> 2.66 us
  other arithmetic: 51.2 us -> 12.5 us
    convert_element_type x1 -> x0, local copies, waits for them, and re-layouts: 52.2 us -> none  [body(): update_rows = (combined * (0.2 * math.sqrt(D))).astype(jnp.bfloat16)]
    unnamed x1 -> x0, other arithmetic: 38.7 us -> none
    unnamed x10 -> x14, local copies, waits for them, and re-layouts: 21 us -> 2.07 us
  transfers between devices with their start and end apart: 2 -> 2, of which waited for: 2 -> 2; matrix products, arithmetic and copies ran while one was open for 1% -> 2% of each run, Pallas kernels for 0% -> 0%
where the time goes in v2:
time: 280 us
  waiting for transfers between devices  127 us (45%)
  blocking collectives  87.2 us (31%)
  matrix products  28.3 us (10%)
  between operations  14.8 us (5%)
  other arithmetic  12.5 us (4%)
  starting transfers between devices  7.45 us (3%)
    all_to_all x1, blocking collectives, body(): lax.all_to_all(jnp.stack(jnp.split(update_rows, lax.axis_size('dp'), axis...  87.2 us
    all_to_all x1, waiting for transfers between devices, body(): lax.all_to_all(narrowed, 'dp', split_axis=0, concat_axis=1, tiled=True)  80.9 us
    psum x1, waiting for transfers between devices, body(): lax.psum(partial_gram.astype(jnp.bfloat16), 'owner').astype(jnp.float32)  45.9 us
    dot_general x1, matrix products, body(): jnp.einsum('mcd,mdr->mcr', normed_gram, once.astype(jnp.bfloat16), prefer...  9.87 us
    dot_general x1, matrix products, body(): jnp.einsum('mcd,mdr->mcr', normed_gram, regrouped, preferred_element_type...  9.86 us
    dot_general x1, matrix products, body(): jnp.einsum('mcr,mdr->mcd', regrouped, regrouped, preferred_element_type=j...  8.55 us
    all_to_all x1, starting transfers between devices, body(): lax.all_to_all(narrowed, 'dp', split_axis=0, concat_axis=1, tiled=True)  7.41 us
  transfers between devices with their start and end apart: 2, of which 2 were waited for; matrix products, arithmetic and copies ran while one was open for 2% of the time, Pallas kernels for 0%

profile of v2, /device:TPU:0, one launch (start us, length us, event | category | flops | bytes accessed | tf_op | source)
XLA Modules:
  0.0 279.6 jit_solution(3642444511742317411)
XLA Ops:
  6.5 5.3 %convert_element_type.32 = bf16[8,128,1792]{2,1,0:T(8,128)(2,1)} convert(f32[8,128,1792]{2,1,0:T(8,128)} %param.2) | non-fusion elementwise | flops 1835008 | bytes 11010048 | tf_op jit(solution)/shard_map/convert_element_type | solution.py:11
  11.9 0.0 copy-start.2
  11.9 7.4 %all-to-all-start = ((bf16[8,128,1792]{2,1,0:T(8,128)(2,1)}), bf16[8,128,1792]{2,1,0:T(8,128)(2,1)}, u32[]{:S(2)}, u32[]{:S(2)}) async-start(bf16[8,128,1792]{2,1,0:T(8,128)(2,1)} %convert_element_type.32), calls=%async_computation | async-start | bytes 7340032 | tf_op jit(solution)/shard_map/all_to_all | solution.py:12
  19.3 0.0 all-reduce.2.cloned.1.call-start
  19.3 0.0 copy-done.2
  19.3 0.6 dynamic_slice.3
  19.9 0.5 iota_compare_fusion.1
  20.5 80.9 %all-to-all-done = bf16[8,128,1792]{2,1,0:T(8,128)(2,1)} async-done(((bf16[8,128,1792]{2,1,0:T(8,128)(2,1)}), bf16[8,128,1792]{2,1,0:T(8,128)(2,1)}, u32[]{:S(2)}, u32[]{:S(2)}) %all-to-all-start) | async-done | bytes 3670048 | tf_op jit(solution)/shard_map/all_to_all | solution.py:12
  101.3 8.6 %convert_bitcast_fusion = bf16[1,1024,1024]{2,1,0:T(8,128)(2,1)} fusion(bf16[1,1024,1,1,1,1,1792]{6,1,5,4,3,2,0:T(8,128)(2,1)} %bitcast.2, pred[1024]{0:T(1024)(128)(4,1)S(1)} %iota_compare_fusion.1), kind=kOutput, calls=%fused_computation.16 | convolution fusion | flops 3760979968 | bytes 5768192 | tf_op jit(solution)/shard_map/mcr,mdr->mcd/dot_general | solution.py:19
  109.9 0.0 all-reduce.2.cloned.1.call-update
  110.5 4.2 %bitcast_select_fusion = bf16[1024,1792]{1,0:T(8,128)(2,1)} fusion(bf16[8,128,1792]{2,1,0:T(8,128)(2,1)} %all-to-all-done, pred[1024]{0:T(1024)(128)(4,1)S(1)} %iota_compare_fusion.1), kind=kLoop, calls=%fused_computation.11 | loop fusion | flops 1835008 | bytes 7341056 | tf_op jit(solution)/shard_map/jit(_where)/select_n | solution.py:18
  114.7 45.9 %all-reduce.2.cloned.1.call-done = bf16[1,1024,1024]{2,1,0:T(8,128)(2,1)} async-done(((bf16[1,1024,1024]{2,1,0:T(8,128)(2,1)}), bf16[1,1024,1024]{2,1,0:T(8,128)(2,1)}) %all-reduce.2.cloned.1.call-update) | async-done | bytes 2097168 | tf_op jit(solution)/shard_map/psum | solution.py:23
  160.5 2.4 fusion
  163.7 0.0 copy-start
  163.7 0.0 copy-start.1
  163.7 9.9 %fusion.2 = f32[1024,1792]{1,0:T(8,128)} fusion(bf16[1,1024,1,1,1,1,1792]{6,1,5,4,3,2,0:T(8,128)(2,1)} %bitcast.2, pred[1024]{0:T(1024)(128)(4,1)S(1)} %iota_compare_fusion.1, bf16[1,1024,1024]{2,1,0:T(8,128)(2,1)} %all-reduce.2.cloned.1.call-done, f32[]{:T(128)} %bitcast.7), kind=kOutput, calls=%fused_computation.7 | convolution fusion | flops 3763077120 | bytes 13108228 | tf_op jit(solution)/shard_map/mcd,mdr->mcr/dot_general | solution.py:29
  173.5 0.0 copy-done
  173.5 0.0 copy-done.1
  173.5 9.9 %fusion.7 = bf16[1,1024,1792]{2,1,0:T(8,128)(2,1)S(1)} fusion(f32[1024,1792]{1,0:T(8,128)} %fusion.2, f32[]{:T(128)} %bitcast.6, f32[]{:T(128)S(6)} %mul.54, bf16[1024,1792]{1,0:T(8,128)(2,1)S(1)} %copy-done, bf16[1,1024,1024]{2,1,0:T(8,128)(2,1)S(1)} %copy-done.1, f32[]{:T(128)} %bitcast.7), kind=kOutput, calls=%fused_computation.14 | convolution fusion | flops 3781427200 | bytes 16777228 | tf_op jit(solution)/shard_map/mcd,mdr->mcr/dot_general | solution.py:32
  183.7 87.2 %all_to_all.20 = bf16[8,1,128,1792]{3,2,1,0:T(8,128)(2,1)S(1)} all-to-all(bf16[8,1,128,1792]{3,2,1,0:T(8,128)(2,1)S(1)} %fusion.11), channel_id=1, replica_groups=mesh['dp'=8,'owner'=4] {'dp'}, dimensions={0} | all-to-all | bytes 7340032 | tf_op jit(solution)/shard_map/all_to_all | solution.py:38
  270.9 1.8 copy.12
  (8 shorter events, 0.3 us)
Async XLA Ops:
  11.9 7.5 %copy-start.2 = (s32[8]{0:T(128)S(1)}, s32[8]{0:T(128)}, u32[]{:S(2)}) copy-start(s32[8]{0:T(128)} %param.3) | copy-start | bytes 100
  11.9 89.5 %all-to-all-start = ((bf16[8,128,1792]{2,1,0:T(8,128)(2,1)}), bf16[8,128,1792]{2,1,0:T(8,128)(2,1)}, u32[]{:S(2)}, u32[]{:S(2)}) async-start(bf16[8,128,1792]{2,1,0:T(8,128)(2,1)} %convert_element_type.32), calls=%async_computation | async-start | bytes 7340032 | tf_op jit(solution)/shard_map/all_to_all | solution.py:12
  19.3 141.2 %all-reduce.2.cloned.1.call-start = ((), (), s32[]{:S(2)}) async-start(), calls=%async_computation.2 | async-start | bytes 4194304 | tf_op jit(solution)/shard_map/psum | solution.py:23
  163.7 9.9 %copy-start = (bf16[1024,1792]{1,0:T(8,128)(2,1)S(1)}, bf16[1024,1792]{1,0:T(8,128)(2,1)}, u32[]{:S(2)}) copy-start(bf16[1024,1792]{1,0:T(8,128)(2,1)} %bitcast_select_fusion) | copy-start | bytes 11010052
  163.7 9.9 %copy-start.1 = (bf16[1,1024,1024]{2,1,0:T(8,128)(2,1)S(1)}, bf16[1,1024,1024]{2,1,0:T(8,128)(2,1)}, u32[]{:S(2)}) copy-start(bf16[1,1024,1024]{2,1,0:T(8,128)(2,1)} %all-reduce.2.cloned.1.call-done) | copy-start | bytes 6291460
Sparse Core Ops, SparseCore 0:
  110.0 50.4 all-reduce.1
